TPU v7x, 32 devices: a whole 2x2x4 slice. The times are simulated.
32 devices in a mesh: dom: 16 (over z, x, core), vec: 2 (over y).
Axes of the slice: x: 2, y: 2, z: 4, core: 2. Of those that a mesh axis runs over, the one named last changes fastest.
Arguments:
- orbitals: bfloat16 [128, 65536], P(None, ('dom', 'vec'))
- projectors: bfloat16 [65536, 512], P('dom', 'vec'), may hold values from -0.0234375 to 0.0234375
- potential: float32 [65536], P(('dom', 'vec')), may hold values from 0 to 2
Outputs:
- filtered: bfloat16 [128, 65536], P(None, ('dom', 'vec'))
All inputs are finite; a program needn't handle non-finite values.
Results may differ from a plain program's by a relative error of at most 0.0052.
Values may be sent and summed in bfloat16 or wider, within the bound.
No kernel may reach another device: no remote copies, remote signals or barrier semaphores. Data moves between devices by JAX's collectives and lax.ppermute only.
A program may use at most 64 MiB of HBM per device.

v0:
```python
import jax
import jax.numpy as jnp
from jax import lax
from jax.sharding import PartitionSpec as P

CENTER = 1.0
HALF_WIDTH = 1.5
EPSILON = 1e-06


def hamiltonian(bands_now, projectors, shifted):
    partial_sum = jnp.dot(
        lax.all_gather(bands_now, "vec", axis=1, tiled=True),
        projectors,
        preferred_element_type=jnp.float32,
    )
    intersection_b = lax.psum(partial_sum, "dom").astype(jnp.bfloat16)
    action_terms = lax.dot_general(
        intersection_b, projectors, (((1,), (1,)), ((), ())), preferred_element_type=jnp.float32
    )
    actions = lax.psum_scatter(action_terms, "vec", scatter_dimension=1, tiled=True)
    return (shifted[None, :] * bands_now.astype(jnp.float32) - actions) / HALF_WIDTH


def chebyshev(bands_now, projectors, shifted):
    first_step = hamiltonian(bands_now, projectors, shifted).astype(jnp.bfloat16)
    return 2.0 * hamiltonian(first_step, projectors, shifted) - bands_now.astype(jnp.float32)


def body(orbitals, projectors, potential):
    local_rows = orbitals.shape[1]
    grid_count = local_rows * lax.axis_size("dom") * lax.axis_size("vec")
    shifted = potential - CENTER
    panel_list = [orbitals]
    seconds = [chebyshev(bands_now, projectors, shifted) for bands_now in panel_list]
    second = seconds[0]
    square_sum = lax.psum(jnp.sum(second * second, axis=1), ("dom", "vec"))
    normed_list = second * lax.rsqrt(square_sum / grid_count + EPSILON)[:, None]
    return normed_list.astype(jnp.bfloat16)


def solution(mesh):
    return jax.shard_map(
        body,
        mesh=mesh,
        in_specs=(P(None, ("dom", "vec")), P("dom", "vec"), P(("dom", "vec"))),
        out_specs=P(None, ("dom", "vec")),
        check_vma=False,
    )
```

profile of v0, /device:TPU:0, one launch (start us, length us, event | category | flops | bytes accessed | tf_op | source)
XLA Modules:
  0.0 294.5 jit_solution(7076762438744303975)
XLA Ops:
  6.5 0.0 copy-start
  6.5 0.0 all-gather.3.cloned.1.call-start
  6.5 0.7 all-gather.3.cloned.1.call-update
  7.3 0.0 reduce-scatter.3.cloned.1.call-start
  7.3 25.6 %all-gather.3.cloned.1.call-done = bf16[128,4096]{1,0:T(8,128)(2,1)} async-done(((bf16[128,2048]{1,0:T(8,128)(2,1)}), bf16[128,4096]{1,0:T(8,128)(2,1)}) %all-gather.3.cloned.1.call-update) | async-done | bytes 1048592 | tf_op jit(solution)/shard_map/all_gather | solution.py:13
  32.9 0.0 copy-done
  32.9 1.7 fusion.7
  34.6 61.8 %all-reduce.2 = bf16[128,256]{1,0:T(8,128)(2,1)S(1)} all-reduce(f32[128,256]{1,0:T(8,128)S(1)} %fusion.7), channel_id=1, replica_groups=mesh['dom'=16,'vec'=2] {'dom'}, use_global_device_ids=true, to_apply=%region_0.0 | all-reduce | flops 32768 | bytes 196608 | tf_op jit(solution)/shard_map/psum | solution.py:17
  96.4 2.2 fusion.10
  98.6 0.0 copy-start.3
  98.6 0.0 copy-start.1
  98.6 0.0 reduce-scatter.3.cloned.1.call-update
  98.6 0.0 all-gather.5.cloned.1.call-start
  98.7 0.6 copy-done.3
  99.3 27.8 %reduce-scatter.3.cloned.1.call-done = f32[128,2048]{1,0:T(8,128)} async-done(((f32[128,4096]{1,0:T(8,128)}), f32[128,2048]{1,0:T(8,128)}) %reduce-scatter.3.cloned.1.call-update) | async-done | bytes 1048592 | tf_op jit(solution)/shard_map/reduce_scatter | solution.py:21
  127.1 0.0 copy-done.1
  127.1 2.2 fusion.2
  129.2 0.0 all-gather.5.cloned.1.call-update
  129.3 0.0 reduce-scatter.5.cloned.1.call-start
  129.3 21.4 %all-gather.5.cloned.1.call-done = bf16[128,4096]{1,0:T(8,128)(2,1)} async-done(((bf16[128,2048]{1,0:T(8,128)(2,1)}), bf16[128,4096]{1,0:T(8,128)(2,1)}) %all-gather.5.cloned.1.call-update) | async-done | bytes 1048592 | tf_op jit(solution)/shard_map/all_gather | solution.py:13
  150.7 1.7 fusion.8
  152.4 61.8 %all-reduce.3 = bf16[128,256]{1,0:T(8,128)(2,1)S(1)} all-reduce(f32[128,256]{1,0:T(8,128)S(1)} %fusion.8), channel_id=1, replica_groups=mesh['dom'=16,'vec'=2] {'dom'}, use_global_device_ids=true, to_apply=%region_2.0 | all-reduce | flops 32768 | bytes 196608 | tf_op jit(solution)/shard_map/psum | solution.py:17
  214.2 2.2 fusion.9
  216.4 0.0 copy-start.2
  216.4 0.0 reduce-scatter.5.cloned.1.call-update
  216.4 28.4 %reduce-scatter.5.cloned.1.call-done = f32[128,2048]{1,0:T(8,128)} async-done(((f32[128,4096]{1,0:T(8,128)}), f32[128,2048]{1,0:T(8,128)}) %reduce-scatter.5.cloned.1.call-update) | async-done | bytes 1048592 | tf_op jit(solution)/shard_map/reduce_scatter | solution.py:21
  244.8 0.0 copy-done.2
  244.8 1.6 multiply_reduce_fusion
  246.4 39.3 %psum.23 = f32[128]{0:T(128)S(1)} all-reduce(f32[128]{0:T(128)S(1)} %multiply_reduce_fusion), channel_id=1, replica_groups=mesh['dom'=16,'vec'=2] {'dom','vec'}, use_global_device_ids=true, to_apply=%region_5.0 | all-reduce | flops 128 | bytes 1024 | tf_op jit(solution)/shard_map/psum | solution.py:37
  285.7 2.3 multiply_convert_fusion
  (2 shorter events, 0.0 us)
Async XLA Ops:
  6.5 26.4 %copy-start = (bf16[4096,256]{1,0:T(8,128)(2,1)S(1)}, bf16[4096,256]{1,0:T(8,128)(2,1)}, u32[]{:S(2)}) copy-start(bf16[4096,256]{1,0:T(8,128)(2,1)} %param.4) | copy-start | bytes 6291460
  6.5 26.4 %all-gather.3.cloned.1.call-start = ((), (), s32[]{:S(2)}) async-start(), calls=%async_computation.2 | async-start | bytes 1572864 | tf_op jit(solution)/shard_map/all_gather | solution.py:13
  7.3 119.8 %reduce-scatter.3.cloned.1.call-start = ((), (), s32[]{:S(2)}) async-start(), calls=%async_computation.3 | async-start | bytes 3145728 | tf_op jit(solution)/shard_map/reduce_scatter | solution.py:21
  98.6 0.7 copy-start.3
  98.6 28.5 %copy-start.1 = (bf16[128,2048]{1,0:T(8,128)(2,1)S(1)}, bf16[128,2048]{1,0:T(8,128)(2,1)}, u32[]{:S(2)}) copy-start(bf16[128,2048]{1,0:T(8,128)(2,1)} %param.3) | copy-start | bytes 1572868
  98.6 52.1 %all-gather.5.cloned.1.call-start = ((), (), s32[]{:S(2)}) async-start(), calls=%async_computation.4 | async-start | bytes 1572864 | tf_op jit(solution)/shard_map/all_gather | solution.py:13
  129.3 115.6 %reduce-scatter.5.cloned.1.call-start = ((), (), s32[]{:S(2)}) async-start(), calls=%async_computation.5 | async-start | bytes 3145728 | tf_op jit(solution)/shard_map/reduce_scatter | solution.py:21
  216.4 28.5 %copy-start.2 = (bf16[128,2048]{1,0:T(8,128)(2,1)S(1)}, bf16[128,2048]{1,0:T(8,128)(2,1)}, u32[]{:S(2)}) copy-start(bf16[128,2048]{1,0:T(8,128)(2,1)} %fusion.2) | copy-start | bytes 1572868
Sparse Core Ops, SparseCore 0:
  8.9 23.9 all-gather.2
  98.7 28.2 reduce-scatter.2
  129.4 21.2 all-gather.4
  216.5 28.2 reduce-scatter.4
where the time goes:
time: 295 us
  blocking collectives  163 us (55%)
  waiting for transfers between devices  104 us (35%)
  between operations  13.2 us (4%)
  matrix products  7.67 us (3%)
  other arithmetic  6.06 us (2%)
    psum x2, blocking collectives, hamiltonian(): intersection_b = lax.psum(partial_sum, 'dom').astype(jnp.bfloat16)  124 us
    reduce_scatter x2, waiting for transfers between devices, hamiltonian(): lax.psum_scatter(action_terms, 'vec', scatter_dimension=1, tiled=True)  56.2 us
    all_gather x2, waiting for transfers between devices, hamiltonian(): lax.all_gather(bands_now, 'vec', axis=1, tiled=True)  47 us
    psum x1, blocking collectives, body(): square_sum = lax.psum(jnp.sum(second * second, axis=1), ('dom', 'vec'))  39.3 us
  transfers between devices with their start and end apart: 4, of which 4 were waited for; matrix products, arithmetic and copies ran while one was open for 0% of the time, Pallas kernels for 0%

commit v1 on v0

--- a/solution.py
+++ b/solution.py
@@ -6,6 +6,7 @@
 CENTER = 1.0
 HALF_WIDTH = 1.5
 EPSILON = 1e-06
+view_the_field = lambda x0, along_axis: jnp.sum(lax.all_gather(x0, axis_name=along_axis), 0)
 
 
 def hamiltonian(bands_now, projectors, shifted):
@@ -14,7 +15,7 @@
         projectors,
         preferred_element_type=jnp.float32,
     )
-    intersection_b = lax.psum(partial_sum, "dom").astype(jnp.bfloat16)
+    intersection_b = view_the_field(partial_sum, along_axis="dom").astype(jnp.bfloat16)
     action_terms = lax.dot_general(
         intersection_b, projectors, (((1,), (1,)), ((), ())), preferred_element_type=jnp.float32
     )

time: 295 us -> 264 us (0.89)
  blocking collectives: 163 us -> 39.3 us
  waiting for transfers between devices: 104 us -> 192 us
  other arithmetic: 6.06 us -> 9.52 us
    psum x2 -> x0, blocking collectives: 124 us -> none  [hamiltonian(): intersection_b = lax.psum(partial_sum, 'dom').astype(jnp.bfloat16)]
    all_gather x0 -> x2, waiting for transfers between devices: none -> 83.1 us  [lax.all_gather(x0, axis_name=along_axis)]
    reduce_scatter x2, waiting for transfers between devices: 56.2 us -> 60.9 us  [hamiltonian(): lax.psum_scatter(action_terms, 'vec', scatter_dimension=1, tiled=True)]
    reduce_sum x0 -> x2, other arithmetic: none -> 3.46 us  [jnp.sum(lax.all_gather(x0, axis_name=along_axis), 0)]
  transfers between devices with their start and end apart: 4 -> 6, of which waited for: 4 -> 6; matrix products, arithmetic and copies ran while one was open for 0% -> 0% of each run, Pallas kernels for 0% -> 0%
where the time goes in v1:
time: 264 us
  waiting for transfers between devices  192 us (73%)
  blocking collectives  39.3 us (15%)
  between operations  13.5 us (5%)
  other arithmetic  9.52 us (4%)
  matrix products  8.93 us (3%)
    all_gather x2, waiting for transfers between devices, lax.all_gather(x0, axis_name=along_axis)  83.1 us
    reduce_scatter x2, waiting for transfers between devices, hamiltonian(): lax.psum_scatter(action_terms, 'vec', scatter_dimension=1, tiled=True)  60.9 us
    all_gather x2, waiting for transfers between devices, hamiltonian(): lax.all_gather(bands_now, 'vec', axis=1, tiled=True)  47 us
    psum x1, blocking collectives, body(): square_sum = lax.psum(jnp.sum(second * second, axis=1), ('dom', 'vec'))  39.3 us
  transfers between devices with their start and end apart: 6, of which 6 were waited for; matrix products, arithmetic and copies ran while one was open for 0% of the time, Pallas kernels for 0%

profile of v1, /device:TPU:0, one launch (start us, length us, event | category | flops | bytes accessed | tf_op | source)
XLA Modules:
  0.0 263.9 jit_solution(17864897146212749493)
XLA Ops:
  6.5 0.0 copy-start
  6.5 0.0 all-gather.7.cloned.1.call-start
  6.5 0.7 all-gather.7.cloned.1.call-update
  7.3 0.0 all-gather.11.cloned.1.call-start
  7.3 25.6 %all-gather.7.cloned.1.call-done = bf16[128,4096]{1,0:T(8,128)(2,1)} async-done(((bf16[128,2048]{1,0:T(8,128)(2,1)}), bf16[128,4096]{1,0:T(8,128)(2,1)}) %all-gather.7.cloned.1.call-update) | async-done | bytes 1048592 | tf_op jit(solution)/shard_map/all_gather | solution.py:14
  32.9 0.0 copy-done
  32.9 2.3 fusion.7
  35.2 0.0 all-gather.11.cloned.1.call-update
  35.3 0.0 reduce-scatter.3.cloned.1.call-start
  35.3 41.6 %all-gather.11.cloned.1.call-done = f32[2048,256]{1,0:T(8,128)} async-done(((f32[128,256]{1,0:T(8,128)}), f32[2048,256]{1,0:T(8,128)}) %all-gather.11.cloned.1.call-update) | async-done | bytes 2097168 | tf_op jit(solution)/shard_map/all_gather | solution.py:9
  76.9 1.7 reduce_sum.27
  78.6 2.1 fusion.10
  80.7 0.0 copy-start.3
  80.7 0.0 copy-start.1
  80.7 0.0 reduce-scatter.3.cloned.1.call-update
  80.8 0.0 all-gather.9.cloned.1.call-start
  80.8 0.6 copy-done.3
  81.4 30.1 %reduce-scatter.3.cloned.1.call-done = f32[128,2048]{1,0:T(8,128)} async-done(((f32[128,4096]{1,0:T(8,128)}), f32[128,2048]{1,0:T(8,128)}) %reduce-scatter.3.cloned.1.call-update) | async-done | bytes 1048592 | tf_op jit(solution)/shard_map/reduce_scatter | solution.py:22
  111.6 0.0 copy-done.1
  111.6 2.2 fusion.2
  113.8 0.0 all-gather.9.cloned.1.call-update
  113.8 0.0 all-gather.13.cloned.1.call-start
  113.8 21.4 %all-gather.9.cloned.1.call-done = bf16[128,4096]{1,0:T(8,128)(2,1)} async-done(((bf16[128,2048]{1,0:T(8,128)(2,1)}), bf16[128,4096]{1,0:T(8,128)(2,1)}) %all-gather.9.cloned.1.call-update) | async-done | bytes 1048592 | tf_op jit(solution)/shard_map/all_gather | solution.py:14
  135.2 2.3 fusion.8
  137.5 0.0 all-gather.13.cloned.1.call-update
  137.6 0.0 reduce-scatter.5.cloned.1.call-start
  137.6 41.6 %all-gather.13.cloned.1.call-done = f32[2048,256]{1,0:T(8,128)} async-done(((f32[128,256]{1,0:T(8,128)}), f32[2048,256]{1,0:T(8,128)}) %all-gather.13.cloned.1.call-update) | async-done | bytes 2097168 | tf_op jit(solution)/shard_map/all_gather | solution.py:9
  179.2 1.7 reduce_sum.28
  180.9 2.1 fusion.9
  183.0 0.0 copy-start.2
  183.0 0.0 reduce-scatter.5.cloned.1.call-update
  183.1 30.8 %reduce-scatter.5.cloned.1.call-done = f32[128,2048]{1,0:T(8,128)} async-done(((f32[128,4096]{1,0:T(8,128)}), f32[128,2048]{1,0:T(8,128)}) %reduce-scatter.5.cloned.1.call-update) | async-done | bytes 1048592 | tf_op jit(solution)/shard_map/reduce_scatter | solution.py:22
  213.8 0.0 copy-done.2
  213.8 1.6 multiply_reduce_fusion
  215.4 39.3 %psum.7 = f32[128]{0:T(128)S(1)} all-reduce(f32[128]{0:T(128)S(1)} %multiply_reduce_fusion), channel_id=1, replica_groups=mesh['dom'=16,'vec'=2] {'dom','vec'}, use_global_device_ids=true, to_apply=%region_5.0 | all-reduce | flops 128 | bytes 1024 | tf_op jit(solution)/shard_map/psum | solution.py:38
  254.7 2.3 multiply_convert_fusion
  (2 shorter events, 0.0 us)
Async XLA Ops:
  6.5 26.4 %copy-start = (bf16[4096,256]{1,0:T(8,128)(2,1)S(1)}, bf16[4096,256]{1,0:T(8,128)(2,1)}, u32[]{:S(2)}) copy-start(bf16[4096,256]{1,0:T(8,128)(2,1)} %param.4) | copy-start | bytes 6291460
  6.5 26.4 %all-gather.7.cloned.1.call-start = ((), (), s32[]{:S(2)}) async-start(), calls=%async_computation.2 | async-start | bytes 1572864 | tf_op jit(solution)/shard_map/all_gather | solution.py:14
  7.3 69.6 %all-gather.11.cloned.1.call-start = ((), (), s32[]{:S(2)}) async-start(), calls=%async_computation.6 | async-start | bytes 2228224 | tf_op jit(solution)/shard_map/all_gather | solution.py:9
  35.3 76.3 %reduce-scatter.3.cloned.1.call-start = ((), (), s32[]{:S(2)}) async-start(), calls=%async_computation.3 | async-start | bytes 3145728 | tf_op jit(solution)/shard_map/reduce_scatter | solution.py:22
  80.7 0.7 copy-start.3
  80.7 30.8 %copy-start.1 = (bf16[128,2048]{1,0:T(8,128)(2,1)S(1)}, bf16[128,2048]{1,0:T(8,128)(2,1)}, u32[]{:S(2)}) copy-start(bf16[128,2048]{1,0:T(8,128)(2,1)} %param.3) | copy-start | bytes 1572868
  80.8 54.4 %all-gather.9.cloned.1.call-start = ((), (), s32[]{:S(2)}) async-start(), calls=%async_computation.4 | async-start | bytes 1572864 | tf_op jit(solution)/shard_map/all_gather | solution.py:14
  113.8 65.4 %all-gather.13.cloned.1.call-start = ((), (), s32[]{:S(2)}) async-start(), calls=%async_computation.7 | async-start | bytes 2228224 | tf_op jit(solution)/shard_map/all_gather | solution.py:9
  137.6 76.3 %reduce-scatter.5.cloned.1.call-start = ((), (), s32[]{:S(2)}) async-start(), calls=%async_computation.5 | async-start | bytes 3145728 | tf_op jit(solution)/shard_map/reduce_scatter | solution.py:22
  183.0 30.8 %copy-start.2 = (bf16[128,2048]{1,0:T(8,128)(2,1)S(1)}, bf16[128,2048]{1,0:T(8,128)(2,1)}, u32[]{:S(2)}) copy-start(bf16[128,2048]{1,0:T(8,128)(2,1)} %fusion.2) | copy-start | bytes 1572868
Sparse Core Ops, SparseCore 0:
  8.9 23.9 all-gather.6
  35.4 41.4 all-gather.10
  80.9 30.6 reduce-scatter.2
  113.9 21.2 all-gather.8
  137.7 41.4 all-gather.12
  183.2 30.6 reduce-scatter.4
